TPU v7x, 256 devices: a whole 4x4x8 slice. The times are simulated.
256 devices in a mesh: row: 8 (over z), col: 16 (over y_lo, x, core), layer: 2 (over y_hi).
Axes of the slice: x: 4, y: 4 (y_hi: 2, y_lo: 2; y = y_hi * 2 + y_lo), z: 8, core: 2. Of those that a mesh axis runs over, the one named last changes fastest.
Arguments:
- left: bfloat16 [8192, 8192], P('row', ('col', 'layer')), may hold values from -6 to 6
- middle: bfloat16 [8192, 8192], P('row', 'col'), may hold values from -0.0625 to 0.0625
- right: bfloat16 [8192, 8192], P('row', 'col'), may hold values from -0.0625 to 0.0625
Outputs:
- product: bfloat16 [8192, 8192], P('row', ('col', 'layer'))
All inputs are finite; a program needn't handle non-finite values.
Results may differ from a plain program's by a relative error of at most 0.0049.
Values may be sent and summed in bfloat16 or wider, within the bound.
A program may use at most 64 MiB of HBM per device.

v0:
```python
import jax
import jax.numpy as jnp
from jax import lax
from jax.sharding import PartitionSpec as P


def split_up(array, dim, size):
    lengths = array.shape
    blocks = array.reshape(*lengths[:dim], size, lengths[dim] // size, *lengths[dim + 1 :])
    return jnp.moveaxis(blocks, dim, 0)


def sum_at_owner(array, axis, dim):
    blocks = split_up(array, dim, lax.axis_size(axis))
    arrived = lax.all_to_all(blocks, axis, split_axis=0, concat_axis=0, tiled=True)
    return arrived.sum(axis=0)


def multiply(left, right):
    width = left.shape[1]
    layers = lax.axis_size("layer")
    layer_index = lax.axis_index("layer")
    columns = right.shape[1]
    groups = right.shape[0] // width // layers
    shaped = right.reshape(groups, layers, width, columns)
    own_rows = lax.dynamic_index_in_dim(shaped, layer_index, 1, keepdims=False).reshape(
        groups * width, columns
    )
    right_all = lax.all_gather(own_rows, "row", axis=0, tiled=True)
    return jnp.dot(
        lax.all_gather(left, "col", axis=1, tiled=True),
        right_all,
        preferred_element_type=jnp.float32,
    )


def per_device(left, middle, right):
    partial_value = multiply(left, middle)
    first = sum_at_owner(partial_value, "layer", 1)
    first = first.astype(jnp.bfloat16)
    second = multiply(first, right)
    return sum_at_owner(second, "layer", 1).astype(jnp.bfloat16)


def solution(mesh):
    return jax.shard_map(
        per_device,
        mesh=mesh,
        in_specs=(P("row", ("col", "layer")), P("row", "col"), P("row", "col")),
        out_specs=P("row", ("col", "layer")),
        check_vma=False,
    )
```

profile of v0, /device:TPU:1, one launch (start us, length us, event | category | flops | bytes accessed | tf_op | source)
XLA Modules:
  0.0 290.7 jit_solution(16866077000397679622)
XLA Ops:
  6.5 0.0 copy-start
  6.5 0.0 all-gather.5.cloned.1.call-start
  6.5 1.2 copy-done
  7.8 0.8 constant_dynamic-slice_fusion.1
  8.6 0.0 all-gather.5.cloned.1.call-update
  8.6 0.0 all-gather.7.cloned.1.call-start
  8.7 0.7 all-gather.7.cloned.1.call-update
  9.4 0.0 all-gather.11.cloned.1.call-start
  9.4 1.9 constant_dynamic-slice_fusion
  11.3 0.0 all-gather.11.cloned.1.call-update
  11.3 0.0 all-gather.9.cloned.1.call-start
  11.4 56.2 %all-gather.5.cloned.1.call-done = bf16[4096,512]{1,0:T(8,128)(2,1)} async-done(((bf16[512,512]{1,0:T(8,128)(2,1)}), bf16[4096,512]{1,0:T(8,128)(2,1)}) %all-gather.5.cloned.1.call-update) | async-done | bytes 4194320 | tf_op jit(solution)/shard_map/all_gather | solution.py:29
  67.5 64.4 %all-gather.7.cloned.1.call-done = bf16[1024,4096]{1,0:T(8,128)(2,1)} async-done(((bf16[1024,256]{1,0:T(8,128)(2,1)}), bf16[1024,4096]{1,0:T(8,128)(2,1)}) %all-gather.7.cloned.1.call-update) | async-done | bytes 8388624 | tf_op jit(solution)/shard_map/all_gather | solution.py:31
  131.9 8.2 %fusion = f32[512,1024]{1,0:T(8,128)S(1)} fusion(bf16[4096,512]{1,0:T(8,128)(2,1)} %all-gather.5.cloned.1.call-done, bf16[1024,4096]{1,0:T(8,128)(2,1)} %all-gather.7.cloned.1.call-done), kind=kOutput, calls=%fused_computation.2 | convolution fusion | flops 4294967296 | bytes 14680064 | tf_op jit(solution)/shard_map/dot_general | solution.py:30
  140.1 28.8 %all_to_all.10 = f32[2,1024,256]{1,2,0:T(8,128)S(1)} all-to-all(f32[2,1024,256]{1,2,0:T(8,128)S(1)} %bitcast.17), channel_id=1, replica_groups=mesh['row'=8,'col'=16,'layer'=2] {'layer'}, dimensions={0} | all-to-all | bytes 4194304 | tf_op jit(solution)/shard_map/all_to_all | solution.py:15
  168.9 1.1 reduce_sum.18
  170.0 0.0 all-gather.9.cloned.1.call-update
  170.0 17.7 %all-gather.11.cloned.1.call-done = bf16[4096,512]{1,0:T(8,128)(2,1)} async-done(((bf16[512,512]{1,0:T(8,128)(2,1)}), bf16[4096,512]{1,0:T(8,128)(2,1)}) %all-gather.11.cloned.1.call-update) | async-done | bytes 4194320 | tf_op jit(solution)/shard_map/all_gather | solution.py:29
  187.7 55.5 %all-gather.9.cloned.1.call-done = bf16[1024,4096]{0,1:T(8,128)(2,1)} async-done(((bf16[1024,256]{0,1:T(8,128)(2,1)}), bf16[1024,4096]{0,1:T(8,128)(2,1)}) %all-gather.9.cloned.1.call-update) | async-done | bytes 8388624 | tf_op jit(solution)/shard_map/all_gather | solution.py:31
  243.2 8.2 %fusion.1 = f32[1024,512]{0,1:T(8,128)S(1)} fusion(bf16[1024,4096]{0,1:T(8,128)(2,1)} %all-gather.9.cloned.1.call-done, bf16[4096,512]{1,0:T(8,128)(2,1)} %all-gather.11.cloned.1.call-done), kind=kOutput, calls=%fused_computation.3 | convolution fusion | flops 4294967296 | bytes 14680064 | tf_op jit(solution)/shard_map/dot_general | solution.py:30
  251.4 29.6 %all_to_all.11 = f32[2,1024,256]{1,2,0:T(8,128)S(1)} all-to-all(f32[2,1024,256]{1,2,0:T(8,128)S(1)} %bitcast.18), channel_id=1, replica_groups=mesh['row'=8,'col'=16,'layer'=2] {'layer'}, dimensions={0} | all-to-all | bytes 4194304 | tf_op jit(solution)/shard_map/all_to_all | solution.py:15
  281.0 1.1 reduce_sum.19
  282.1 2.0 copy.4
Async XLA Ops:
  6.5 1.2 copy-start
  6.5 61.0 %all-gather.5.cloned.1.call-start = ((), (), s32[]{:S(2)}) async-start(), calls=%async_computation.2 | async-start | bytes 4718592 | tf_op jit(solution)/shard_map/all_gather | solution.py:29
  8.6 123.3 %all-gather.7.cloned.1.call-start = ((), (), s32[]{:S(2)}) async-start(), calls=%async_computation.3 | async-start | bytes 8912896 | tf_op jit(solution)/shard_map/all_gather | solution.py:31
  9.4 178.3 %all-gather.11.cloned.1.call-start = ((), (), s32[]{:S(2)}) async-start(), calls=%async_computation.5 | async-start | bytes 4718592 | tf_op jit(solution)/shard_map/all_gather | solution.py:29
  11.3 231.9 %all-gather.9.cloned.1.call-start = ((), (), s32[]{:S(2)}) async-start(), calls=%async_computation.4 | async-start | bytes 8912896 | tf_op jit(solution)/shard_map/all_gather | solution.py:31
Sparse Core Ops, SparseCore 0:
  9.1 58.3 all-gather.4
  69.3 62.5 all-gather.6
  133.7 53.9 all-gather.10
  189.4 53.7 all-gather.8
where the time goes:
time: 291 us
  waiting for transfers between devices  194 us (67%)
  blocking collectives  58.3 us (20%)
  matrix products  16.5 us (6%)
  between operations  13.1 us (5%)
  local copies, waits for them, and re-layouts  5.97 us (2%)
    all_gather x2, waiting for transfers between devices, multiply(): lax.all_gather(left, 'col', axis=1, tiled=True)  120 us
    all_gather x2, waiting for transfers between devices, multiply(): right_all = lax.all_gather(own_rows, 'row', axis=0, tiled=True)  73.8 us
    all_to_all x2, blocking collectives, sum_at_owner(): lax.all_to_all(blocks, axis, split_axis=0, concat_axis=0, tiled=True)  58.3 us
    dot_general x2, matrix products, multiply(): jnp.dot(lax.all_gather(left, 'col', axis=1, tiled=True), right_all, prefe...  16.5 us
  transfers between devices with their start and end apart: 4, of which 4 were waited for; matrix products, arithmetic and copies ran while one was open for 4% of the time, Pallas kernels for 0%

commit v1 on v0

--- a/solution.py
+++ b/solution.py
@@ -28,7 +28,9 @@
     )
     right_all = lax.all_gather(own_rows, "row", axis=0, tiled=True)
     return jnp.dot(
-        lax.all_gather(left, "col", axis=1, tiled=True),
+        jnp.concatenate(
+            lax.all_to_all(jnp.stack([left] * lax.axis_size("col")), "col", 0, 0), axis=1
+        ),
         right_all,
         preferred_element_type=jnp.float32,
     )

time: 291 us -> 363 us (1.25)
  local copies, waits for them, and re-layouts: 5.97 us -> 36.6 us
  waiting for transfers between devices: 194 us -> 223 us
  starting transfers between devices: 0.12 us -> 14.1 us
    all_to_all x0 -> x2, waiting for transfers between devices: none -> 165 us  [multiply(): lax.all_to_all(jnp.stack([left] * lax.axis_size('col')), 'col', 0, 0)]
    all_gather x2 -> x0, waiting for transfers between devices: 120 us -> none  [multiply(): lax.all_gather(left, 'col', axis=1, tiled=True)]
    reshape x0 -> x3, local copies, waits for them, and re-layouts: none -> 25.9 us  [the longest x2 24.9 us: multiply(): jnp.concatenate(lax.all_to_all(jnp.stack([left] * lax.axis_size('col')),...]
    all_gather x2, waiting for transfers between devices: 73.8 us -> 58 us  [multiply(): right_all = lax.all_gather(own_rows, 'row', axis=0, tiled=True)]
    all_to_all x0 -> x2, starting transfers between devices: none -> 14 us  [multiply(): lax.all_to_all(jnp.stack([left] * lax.axis_size('col')), 'col', 0, 0)]
    another operation x0 -> x2, local copies, waits for them, and re-layouts: none -> 8.33 us  [multiply(): jnp.stack([left] * lax.axis_size('col'))]
  transfers between devices with their start and end apart: 4 -> 4, of which waited for: 4 -> 3; matrix products, arithmetic and copies ran while one was open for 4% -> 7% of each run, Pallas kernels for 0% -> 0%
where the time goes in v1:
time: 363 us; the launch traced here: 361 us
  waiting for transfers between devices  223 us (61%)
  blocking collectives  56.9 us (16%)
  local copies, waits for them, and re-layouts  36.6 us (10%)
  matrix products  16.5 us (5%)
  starting transfers between devices  14.1 us (4%)
  between operations  13.5 us (4%)
    all_to_all x2, waiting for transfers between devices, multiply(): lax.all_to_all(jnp.stack([left] * lax.axis_size('col')), 'col', 0, 0)  165 us
    all_gather x2, waiting for transfers between devices, multiply(): right_all = lax.all_gather(own_rows, 'row', axis=0, tiled=True)  58 us
    all_to_all x2, blocking collectives, sum_at_owner(): lax.all_to_all(blocks, axis, split_axis=0, concat_axis=0, tiled=True)  56.9 us
    reshape x2, local copies, waits for them, and re-layouts, multiply(): jnp.concatenate(lax.all_to_all(jnp.stack([left] * lax.axis_size('col')),...  24.9 us
    dot_general x2, matrix products, multiply(): jnp.dot(jnp.concatenate(lax.all_to_all(jnp.stack([left] * lax.axis_size('...  16.5 us
    all_to_all x2, starting transfers between devices, multiply(): lax.all_to_all(jnp.stack([left] * lax.axis_size('col')), 'col', 0, 0)  14 us
    another operation x2, local copies, waits for them, and re-layouts, multiply(): jnp.stack([left] * lax.axis_size('col'))  8.33 us
  transfers between devices with their start and end apart: 4, of which 3 were waited for; matrix products, arithmetic and copies ran while one was open for 7% of the time, Pallas kernels for 0%

profile of v1, /device:TPU:1, one launch (start us, length us, event | category | flops | bytes accessed | tf_op | source)
XLA Modules:
  0.0 361.3 jit_solution(17670917914619328528)
XLA Ops:
  6.5 0.0 copy-start
  6.5 1.3 copy.7
  7.9 4.3 %stack.4 = bf16[16,1024,256]{1,2,0:T(8,128)(2,1)} broadcast(bf16[1024,256]{0,1:T(8,128)(2,1)S(1)} %copy.7), dimensions={1,2} | broadcast | bytes 8912896 | tf_op jit(solution)/shard_map/stack | solution.py:32
  12.2 7.7 %all-to-all-start = ((bf16[16,1024,256]{1,2,0:T(8,128)(2,1)}), bf16[16,1024,256]{1,2,0:T(8,128)(2,1)}, u32[]{:S(2)}, u32[]{:S(2)}) async-start(bf16[16,1024,256]{1,2,0:T(8,128)(2,1)} %stack.4), calls=%async_computation | async-start | bytes 16777216 | tf_op jit(solution)/shard_map/all_to_all | solution.py:32
  19.8 0.0 all-gather.3.cloned.1.call-start
  19.9 0.0 copy-done
  19.9 0.8 constant_dynamic-slice_fusion.1
  20.7 0.0 all-gather.3.cloned.1.call-update
  20.8 58.0 %all-gather.3.cloned.1.call-done = bf16[4096,512]{1,0:T(8,128)(2,1)} async-done(((bf16[512,512]{1,0:T(8,128)(2,1)}), bf16[4096,512]{1,0:T(8,128)(2,1)}) %all-gather.3.cloned.1.call-update) | async-done | bytes 4194320 | tf_op jit(solution)/shard_map/all_gather | solution.py:29
  78.7 53.4 %all-to-all-done = bf16[16,1024,256]{1,2,0:T(8,128)(2,1)} async-done(((bf16[16,1024,256]{1,2,0:T(8,128)(2,1)}), bf16[16,1024,256]{1,2,0:T(8,128)(2,1)}, u32[]{:S(2)}, u32[]{:S(2)}) %all-to-all-start) | async-done | bytes 8388640 | tf_op jit(solution)/shard_map/all_to_all | solution.py:32
  132.1 8.2 %fusion = f32[512,1024]{1,0:T(8,128)S(1)} fusion(bf16[4096,512]{1,0:T(8,128)(2,1)} %all-gather.3.cloned.1.call-done, bf16[1024,4096]{0,1:T(8,128)(2,1)} %bitcast.3), kind=kOutput, calls=%fused_computation.3 | convolution fusion | flops 4294967296 | bytes 14680064 | tf_op jit(solution)/shard_map/dot_general | solution.py:30
  140.4 28.6 %all_to_all.20 = f32[2,1024,256]{1,2,0:T(8,128)S(1)} all-to-all(f32[2,1024,256]{1,2,0:T(8,128)S(1)} %bitcast.23), channel_id=1, replica_groups=mesh['row'=8,'col'=16,'layer'=2] {'layer'}, dimensions={0} | all-to-all | bytes 4194304 | tf_op jit(solution)/shard_map/all_to_all | solution.py:15
  168.9 0.2 reduce_sum.18
  169.1 0.2 copy.8
  169.3 4.0 %stack.5 = bf16[16,1024,256]{2,1,0:T(8,128)(2,1)} broadcast(bf16[1024,256]{1,0:T(8,128)(2,1)S(1)} %copy.8), dimensions={1,2} | broadcast | bytes 8912896 | tf_op jit(solution)/shard_map/stack | solution.py:32
  173.4 0.0 copy-start.2
  173.4 6.3 %all-to-all-start.2 = ((bf16[16,1024,256]{2,1,0:T(8,128)(2,1)}), bf16[16,1024,256]{2,1,0:T(8,128)(2,1)}, u32[]{:S(2)}, u32[]{:S(2)}) async-start(bf16[16,1024,256]{2,1,0:T(8,128)(2,1)} %stack.5), calls=%async_computation.2 | async-start | bytes 16777216 | tf_op jit(solution)/shard_map/all_to_all | solution.py:32
  179.7 0.0 all-gather.5.cloned.1.call-start
  179.7 0.0 copy-done.2
  179.8 1.0 copy.11
  180.8 0.0 all-gather.5.cloned.1.call-update
  180.8 111.1 %all-to-all-done.2 = bf16[16,1024,256]{2,1,0:T(8,128)(2,1)} async-done(((bf16[16,1024,256]{2,1,0:T(8,128)(2,1)}), bf16[16,1024,256]{2,1,0:T(8,128)(2,1)}, u32[]{:S(2)}, u32[]{:S(2)}) %all-to-all-start.2) | async-done | bytes 8388640 | tf_op jit(solution)/shard_map/all_to_all | solution.py:32
  292.0 11.4 %copy.9 = bf16[1024,16,256]{2,1,0:T(8,128)(2,1)} copy(bf16[1024,16,256]{2,0,1:T(8,128)(2,1)} %bitcast.7) | data formatting | bytes 16777216 | tf_op jit(solution)/shard_map/reshape | solution.py:31
  303.4 13.5 %reshape.44 = bf16[1024,4096,1]{1,0,2:T(8,128)(2,1)} reshape(bf16[1024,16,256]{2,1,0:T(8,128)(2,1)} %copy.9) | data formatting | bytes 16777216 | tf_op jit(solution)/shard_map/reshape | solution.py:31
  316.8 0.0 all-gather.5.cloned.1.call-done
  316.8 0.0 copy-start.1
  316.9 8.3 %convolution_bitcast_fusion = f32[2,1024,256]{2,1,0:T(8,128)S(1)} fusion(bf16[1024,4096,1]{1,0,2:T(8,128)(2,1)} %reshape.44, bf16[2,256,4096]{2,1,0:T(8,128)(2,1)} %bitcast.27), kind=kOutput, calls=%fused_computation | convolution fusion | flops 4294967296 | bytes 14680064 | tf_op jit(solution)/shard_map/dot_general | solution.py:30
  325.1 28.3 %all_to_all.21 = f32[2,1024,256]{2,1,0:T(8,128)S(1)} all-to-all(f32[2,1024,256]{2,1,0:T(8,128)S(1)} %convolution_bitcast_fusion), channel_id=1, replica_groups=mesh['row'=8,'col'=16,'layer'=2] {'layer'}, dimensions={0} | all-to-all | bytes 4194304 | tf_op jit(solution)/shard_map/all_to_all | solution.py:15
  353.4 1.1 reduce_sum.19
  354.5 0.0 copy-done.1
  (1 shorter events, 0.0 us)
Async XLA Ops:
  6.5 13.4 %copy-start = (bf16[1024,512]{1,0:T(8,128)(2,1)S(1)}, bf16[1024,512]{1,0:T(8,128)(2,1)}, u32[]{:S(2)}) copy-start(bf16[1024,512]{1,0:T(8,128)(2,1)} %param.4) | copy-start | bytes 3145732
  12.2 120.0 %all-to-all-start = ((bf16[16,1024,256]{1,2,0:T(8,128)(2,1)}), bf16[16,1024,256]{1,2,0:T(8,128)(2,1)}, u32[]{:S(2)}, u32[]{:S(2)}) async-start(bf16[16,1024,256]{1,2,0:T(8,128)(2,1)} %stack.4), calls=%async_computation | async-start | bytes 16777216 | tf_op jit(solution)/shard_map/all_to_all | solution.py:32
  19.8 58.9 %all-gather.3.cloned.1.call-start = ((), (), s32[]{:S(2)}) async-start(), calls=%async_computation.4 | async-start | bytes 4718592 | tf_op jit(solution)/shard_map/all_gather | solution.py:29
  173.4 6.4 %copy-start.2 = (bf16[1024,512]{1,0:T(8,128)(2,1)S(1)}, bf16[1024,512]{1,0:T(8,128)(2,1)}, u32[]{:S(2)}) copy-start(bf16[1024,512]{1,0:T(8,128)(2,1)} %param.5) | copy-start | bytes 3145732
  173.4 118.6 %all-to-all-start.2 = ((bf16[16,1024,256]{2,1,0:T(8,128)(2,1)}), bf16[16,1024,256]{2,1,0:T(8,128)(2,1)}, u32[]{:S(2)}, u32[]{:S(2)}) async-start(bf16[16,1024,256]{2,1,0:T(8,128)(2,1)} %stack.5), calls=%async_computation.2 | async-start | bytes 16777216 | tf_op jit(solution)/shard_map/all_to_all | solution.py:32
  179.7 137.1 %all-gather.5.cloned.1.call-start = ((), (), s32[]{:S(2)}) async-start(), calls=%async_computation.5 | async-start | bytes 4718592 | tf_op jit(solution)/shard_map/all_gather | solution.py:29
  316.8 37.7 %copy-start.1 = (bf16[1024,512]{1,0:T(8,128)(2,1)S(1)}, bf16[1024,512]{1,0:T(8,128)(2,1)}, u32[]{:S(2)}) copy-start(bf16[1024,512]{1,0:T(8,128)(2,1)} %param.4) | copy-start | bytes 3145732
Sparse Core Ops, SparseCore 0:
  22.4 56.2 all-gather.2
  182.3 55.7 all-gather.4
